TPU v7x, 32 devices: a whole 2x2x4 slice. The times are simulated.
32 devices in a mesh: task: 4 (over x, core), param: 8 (over z, y).
Axes of the slice: x: 2, y: 2, z: 4, core: 2. Of those that a mesh axis runs over, the one named last changes fastest.
Arguments:
- acts: bfloat16 [128, 3584], replicated, may hold values from -6 to 6
- out_grads: bfloat16 [4, 128, 10240], P('task', None, 'param'), may hold values from -12 to 12
- order: int32 [4], replicated, may hold values from 0 to 3, each once
Outputs:
- update: float32 [3584, 10240], P('task', 'param')
- weights: float32 [4], replicated
All inputs are finite; a program needn't handle non-finite values.
Results may differ from a plain program's by a relative error of at most 0.0029.
Values may be sent and summed in bfloat16 or wider, within the bound.
A program may use at most 64 MiB of HBM per device.

v0:
```python
import jax
import jax.numpy as jnp
from jax import lax
from jax.sharding import PartitionSpec as P


def task_grads(acts_part, blocks):
    return jnp.einsum("td,ktc->kdc", acts_part, blocks, preferred_element_type=jnp.float32).astype(
        jnp.bfloat16
    )


def pcgrad_weights(gram, order):
    count = gram.shape[0]
    ids = jnp.arange(count, dtype=jnp.int32)

    def turn(step, mix):
        target = order[step]
        column = gram[:, target]
        onehot = (ids == target).astype(jnp.float32)
        dots = jnp.dot(mix, column, precision=lax.Precision.HIGHEST)
        scale = jnp.sum(column * onehot) + 1e-06
        change = jnp.minimum(dots, 0.0) / scale * (1.0 - onehot)
        return mix - change[:, None] * onehot[None, :]

    mix = lax.fori_loop(0, count, turn, jnp.eye(count, dtype=jnp.float32))
    return jnp.sum(mix, axis=0)


def shards(acts, out_grads, order):
    local = out_grads.shape[0]
    groups = lax.axis_size("task")
    group_id = lax.axis_index("task")
    total_tasks = local * groups
    part_rows = acts.shape[1] // groups
    acts_rows = lax.dynamic_slice_in_dim(acts, group_id * part_rows, part_rows, 1)
    everyone = lax.all_gather(out_grads, "task", axis=0, tiled=True)
    row_grads = task_grads(acts_rows, everyone)
    flat = row_grads.reshape(total_tasks, -1)
    partial_gram = jnp.dot(flat, flat.T, preferred_element_type=jnp.float32)
    gram = lax.psum(partial_gram, ("task", "param"))
    weights = pcgrad_weights(gram, order)
    combined = jnp.einsum(
        "k,ktc->tc", weights, everyone.astype(jnp.float32), precision=lax.Precision.HIGHEST
    ).astype(jnp.bfloat16)
    update = lax.dot_general(
        acts_rows, combined, (((0,), (0,)), ((), ())), preferred_element_type=jnp.float32
    )
    return (update, weights)


def solution(mesh):
    in_specs = (P(), P("task", None, "param"), P())
    out_specs = (P("task", "param"), P())
    return jax.shard_map(shards, mesh=mesh, in_specs=in_specs, out_specs=out_specs, check_vma=False)
```

profile of v0, /device:TPU:0, one launch (start us, length us, event | category | flops | bytes accessed | tf_op | source)
XLA Modules:
  0.0 130.1 jit_solution(3699769488526502229)
XLA Ops:
  7.2 0.0 copy-start
  7.2 0.0 all-gather.2.cloned.1.call-start
  7.2 0.7 all-gather.2.cloned.1.call-update
  7.9 22.5 %all-gather.2.cloned.1.call-done = bf16[4,128,1280]{2,1,0:T(8,128)(2,1)} async-done(((bf16[1,128,1280]{2,1,0:T(8,128)(2,1)}), bf16[4,128,1280]{2,1,0:T(8,128)(2,1)}) %all-gather.2.cloned.1.call-update) | async-done | bytes 1310736 | tf_op jit(solution)/shard_map/all_gather | solution.py:37
  30.5 0.0 copy-done
  30.5 3.9 %convolution_convert_fusion = bf16[896,4,1280]{2,0,1:T(8,128)(2,1)S(1)} fusion(bf16[4,128,1280]{2,1,0:T(8,128)(2,1)} %all-gather.2.cloned.1.call-done, bf16[128,3584]{1,0:T(8,128)(2,1)S(1)} %copy-done, s32[]{:T(128)S(6)} %select_n.15), kind=kOutput, calls=%fused_computation.10 | convolution fusion | flops 1178992640 | bytes 10715140 | tf_op jit(solution)/shard_map/td,ktc->kdc/dot_general | solution.py:8
  34.4 0.0 copy-start.3
  34.4 0.0 copy-start.1
  34.4 20.1 %fusion.9 = f32[4,4]{1,0:T(4,128)S(1)} fusion(bf16[896,4,1280]{2,0,1:T(8,128)(2,1)S(1)} %convolution_convert_fusion), kind=kOutput, calls=%fused_computation.15 | convolution fusion | flops 36700160 | bytes 9175104 | tf_op jit(solution)/shard_map/dot_general | solution.py:40
  54.4 39.3 %psum.7 = f32[4,4]{1,0:T(4,128)S(1)} all-reduce(f32[4,4]{1,0:T(4,128)S(1)} %fusion.9), channel_id=1, replica_groups=mesh['task'=4,'param'=8] {'task','param'}, use_global_device_ids=true, to_apply=%region_0.0 | all-reduce | flops 16 | bytes 128 | tf_op jit(solution)/shard_map/psum | solution.py:41
  93.7 0.1 copy.6
  93.8 0.0 copy-done.3
  93.8 23.9 %while.14 = (s32[]{:T(128)}, f32[4,4]{1,0:T(4,128)S(1)}, s32[4]{0:T(128)S(1)}, f32[4,4]{0,1:T(4,128)S(1)}, s32[]{:T(128)}, /*index=5*/s32[]{:T(128)}, s32[]{:T(128)}, f32[]{:T(128)}) while((s32[]{:T(128)}, f32[4,4]{1,0:T(4,128)S(1)}, s32[4]{0:T(128)S(1)}, f32[4,4]{0,1:T(4,128)S(1)}, s32[]{:T(128)}, /*index=5*/s32[]{:T(128)}, ...), condition=%wide.region_3.0_spmd.clone, body=%wide.region_1.0_spmd.clone.sunk | while | flops 273 | bytes 2939 | solution.py:26
  93.8 0.6 dynamic_slice.35
  96.4 1.3 fusion.24
  98.3 0.8 fusion.25
  99.1 0.7 compare_convert_fusion.2
  99.7 0.1 multiply_subtract_fusion.2
  99.8 0.6 dynamic_slice.35
  102.3 1.3 fusion.24
  104.3 0.8 fusion.25
  105.0 0.7 compare_convert_fusion.2
  105.7 0.1 multiply_subtract_fusion.2
  105.8 0.6 dynamic_slice.35
  108.3 1.3 fusion.24
  110.2 0.8 fusion.25
  111.0 0.7 compare_convert_fusion.2
  111.7 0.1 multiply_subtract_fusion.2
  111.7 0.6 dynamic_slice.35
  114.3 1.3 fusion.24
  116.2 0.8 fusion.25
  117.0 0.7 compare_convert_fusion.2
  117.6 0.1 multiply_subtract_fusion.2
  117.7 0.0 copy-done.1
  117.7 0.0 copy-start.2
  117.7 2.5 %fusion.7 = bf16[1,128,1280]{2,0,1:T(2,128)(2,1)S(1)} fusion(bf16[4,128,1280]{2,1,0:T(8,128)(2,1)S(1)} %copy-done.1, f32[4]{0:T(128)S(1)} %reduce_sum.22), kind=kOutput, calls=%fused_computation.13 | convolution fusion | flops 7864320 | bytes 1638416 | tf_op jit(solution)/shard_map/k,ktc->tc/dot_general | solution.py:43
  120.3 2.9 %fusion.10 = f32[896,1280]{1,0:T(8,128)} fusion(bf16[1,128,1280]{2,0,1:T(2,128)(2,1)S(1)} %fusion.7, bf16[128,3584]{1,0:T(8,128)(2,1)S(1)} %copy-done, s32[]{:T(128)S(6)} %select_n.15), kind=kOutput, calls=%fused_computation.17 | convolution fusion | flops 293601280 | bytes 5472260 | tf_op jit(solution)/shard_map/dot_general | solution.py:46
  123.2 0.0 copy-done.2
  (2 shorter events, 0.0 us)
Async XLA Ops:
  7.2 23.3 %copy-start = (bf16[128,3584]{1,0:T(8,128)(2,1)S(1)}, bf16[128,3584]{1,0:T(8,128)(2,1)}, u32[]{:S(2)}) copy-start(bf16[128,3584]{1,0:T(8,128)(2,1)} %param.5) | copy-start | bytes 2752516
  7.2 23.3 %all-gather.2.cloned.1.call-start = ((), (), s32[]{:S(2)}) async-start(), calls=%async_computation | async-start | bytes 1638400 | tf_op jit(solution)/shard_map/all_gather | solution.py:37
  34.4 59.5 %copy-start.3 = (s32[4]{0:T(128)S(1)}, s32[4]{0:T(128)}, u32[]{:S(2)}) copy-start(s32[4]{0:T(128)} %param.7) | copy-start | bytes 52
  34.4 83.4 %copy-start.1 = (bf16[4,128,1280]{2,1,0:T(8,128)(2,1)S(1)}, bf16[4,128,1280]{2,1,0:T(8,128)(2,1)}, u32[]{:S(2)}) copy-start(bf16[4,128,1280]{2,1,0:T(8,128)(2,1)} %all-gather.2.cloned.1.call-done) | copy-start | bytes 3932164
  117.7 5.5 %copy-start.2 = (f32[4]{0:T(128)}, f32[4]{0:T(128)S(1)}, u32[]{:S(2)}) copy-start(f32[4]{0:T(128)S(1)} %reduce_sum.22) | copy-start | bytes 52
Sparse Core Ops, SparseCore 0:
  9.5 20.8 all-gather.1
where the time goes:
time: 131 us; the launch traced here: 130 us
  blocking collectives  39.3 us (30%)
  matrix products  32.5 us (25%)
  waiting for transfers between devices  23.2 us (18%)
  between operations  14.1 us (11%)
  loops' own time  10.4 us (8%)
  other arithmetic  8.09 us (6%)
  local copies, waits for them, and re-layouts  2.45 us (2%)
    psum x1, blocking collectives, shards(): gram = lax.psum(partial_gram, ('task', 'param'))  39.3 us
    all_gather x1, waiting for transfers between devices, shards(): everyone = lax.all_gather(out_grads, 'task', axis=0, tiled=True)  22.5 us
    dot_general x1, matrix products, shards(): partial_gram = jnp.dot(flat, flat.T, preferred_element_type=jnp.float32)  20.1 us
    another operation x1, loops' own time, pcgrad_weights(): mix = lax.fori_loop(0, count, turn, jnp.eye(count, dtype=jnp.float32))  10.4 us
    reduce_sum x4, other arithmetic, turn(): scale = jnp.sum(column * onehot) + 1e-06  5.13 us
    dot_general x1, matrix products, task_grads(): jnp.einsum('td,ktc->kdc', acts_part, blocks, preferred_element_type=jnp.f...  3.88 us
    dot_general x4, matrix products, turn(): dots = jnp.dot(mix, column, precision=lax.Precision.HIGHEST)  3.12 us
    dot_general x1, matrix products, shards(): lax.dot_general(acts_rows, combined, (((0,), (0,)), ((), ())), preferred_...  2.94 us
  transfers between devices with their start and end apart: 1, of which 1 were waited for; matrix products, arithmetic and copies ran while one was open for 0% of the time, Pallas kernels for 0%

commit v1 on v0

--- a/solution.py
+++ b/solution.py
@@ -38,7 +38,7 @@
     row_grads = task_grads(acts_rows, everyone)
     flat = row_grads.reshape(total_tasks, -1)
     partial_gram = jnp.dot(flat, flat.T, preferred_element_type=jnp.float32)
-    gram = lax.psum(partial_gram, ("task", "param"))
+    gram = lax.psum(lax.psum(partial_gram, "param"), "task")
     weights = pcgrad_weights(gram, order)
     combined = jnp.einsum(
         "k,ktc->tc", weights, everyone.astype(jnp.float32), precision=lax.Precision.HIGHEST

time: 131 us -> 118 us (0.901)
  blocking collectives: 39.3 us -> 27.3 us
    psum x1 -> x2, blocking collectives: 39.3 us -> 27.3 us  [shards(): gram = lax.psum(lax.psum(partial_gram, 'param'), 'task')]
where the time goes in v1:
time: 118 us
  matrix products  32.5 us (28%)
  blocking collectives  27.3 us (23%)
  waiting for transfers between devices  23.2 us (20%)
  between operations  14.1 us (12%)
  loops' own time  10.4 us (9%)
  other arithmetic  8.09 us (7%)
  local copies, waits for them, and re-layouts  2.45 us (2%)
    psum x2, blocking collectives, shards(): gram = lax.psum(lax.psum(partial_gram, 'param'), 'task')  27.3 us
    all_gather x1, waiting for transfers between devices, shards(): everyone = lax.all_gather(out_grads, 'task', axis=0, tiled=True)  22.5 us
    dot_general x1, matrix products, shards(): partial_gram = jnp.dot(flat, flat.T, preferred_element_type=jnp.float32)  20.1 us
    another operation x1, loops' own time, pcgrad_weights(): mix = lax.fori_loop(0, count, turn, jnp.eye(count, dtype=jnp.float32))  10.4 us
    reduce_sum x4, other arithmetic, turn(): scale = jnp.sum(column * onehot) + 1e-06  5.13 us
    dot_general x1, matrix products, task_grads(): jnp.einsum('td,ktc->kdc', acts_part, blocks, preferred_element_type=jnp.f...  3.88 us
    dot_general x4, matrix products, turn(): dots = jnp.dot(mix, column, precision=lax.Precision.HIGHEST)  3.12 us
    dot_general x1, matrix products, shards(): lax.dot_general(acts_rows, combined, (((0,), (0,)), ((), ())), preferred_...  2.94 us
  transfers between devices with their start and end apart: 1, of which 1 were waited for; matrix products, arithmetic and copies ran while one was open for 0% of the time, Pallas kernels for 0%

profile of v1, /device:TPU:0, one launch (start us, length us, event | category | flops | bytes accessed | tf_op | source)
XLA Modules:
  0.0 118.1 jit_solution(1607498618588159147)
XLA Ops:
  7.2 0.0 copy-start
  7.2 0.0 all-gather.2.cloned.1.call-start
  7.2 0.7 all-gather.2.cloned.1.call-update
  7.9 22.5 %all-gather.2.cloned.1.call-done = bf16[4,128,1280]{2,1,0:T(8,128)(2,1)} async-done(((bf16[1,128,1280]{2,1,0:T(8,128)(2,1)}), bf16[4,128,1280]{2,1,0:T(8,128)(2,1)}) %all-gather.2.cloned.1.call-update) | async-done | bytes 1310736 | tf_op jit(solution)/shard_map/all_gather | solution.py:37
  30.5 0.0 copy-done
  30.5 3.9 %convolution_convert_fusion = bf16[896,4,1280]{2,0,1:T(8,128)(2,1)S(1)} fusion(bf16[4,128,1280]{2,1,0:T(8,128)(2,1)} %all-gather.2.cloned.1.call-done, bf16[128,3584]{1,0:T(8,128)(2,1)S(1)} %copy-done, s32[]{:T(128)S(6)} %select_n.15), kind=kOutput, calls=%fused_computation.10 | convolution fusion | flops 1178992640 | bytes 10715140 | tf_op jit(solution)/shard_map/td,ktc->kdc/dot_general | solution.py:8
  34.4 0.0 copy-start.3
  34.4 0.0 copy-start.1
  34.4 20.1 %fusion.9 = f32[4,4]{1,0:T(4,128)S(1)} fusion(bf16[896,4,1280]{2,0,1:T(8,128)(2,1)S(1)} %convolution_convert_fusion), kind=kOutput, calls=%fused_computation.15 | convolution fusion | flops 36700160 | bytes 9175104 | tf_op jit(solution)/shard_map/dot_general | solution.py:40
  54.4 21.4 %psum.14 = f32[4,4]{1,0:T(4,128)S(1)} all-reduce(f32[4,4]{1,0:T(4,128)S(1)} %fusion.9), channel_id=1, replica_groups=mesh['task'=4,'param'=8] {'param'}, use_global_device_ids=true, to_apply=%region_0.0 | all-reduce | flops 16 | bytes 128 | tf_op jit(solution)/shard_map/psum | solution.py:41
  75.8 5.9 %psum.15 = f32[4,4]{1,0:T(4,128)S(1)} all-reduce(f32[4,4]{1,0:T(4,128)S(1)} %psum.14), channel_id=1, replica_groups=mesh['task'=4,'param'=8] {'task'}, use_global_device_ids=true, to_apply=%region_1.0 | all-reduce | flops 16 | bytes 128 | tf_op jit(solution)/shard_map/psum | solution.py:41
  81.7 0.1 copy.6
  81.8 0.0 copy-done.3
  81.8 23.9 %while.14 = (s32[]{:T(128)}, f32[4,4]{1,0:T(4,128)S(1)}, s32[4]{0:T(128)S(1)}, f32[4,4]{0,1:T(4,128)S(1)}, s32[]{:T(128)}, /*index=5*/s32[]{:T(128)}, s32[]{:T(128)}, f32[]{:T(128)}) while((s32[]{:T(128)}, f32[4,4]{1,0:T(4,128)S(1)}, s32[4]{0:T(128)S(1)}, f32[4,4]{0,1:T(4,128)S(1)}, s32[]{:T(128)}, /*index=5*/s32[]{:T(128)}, ...), condition=%wide.region_4.0_spmd.clone, body=%wide.region_2.0_spmd.clone.sunk | while | flops 273 | bytes 2939 | solution.py:26
  81.8 0.6 dynamic_slice.35
  84.4 1.3 %fusion.24 = f32[]{:T(128)} fusion(s32[]{:T(128)} %bitcast.36, f32[4,4]{0,1:T(4,128)S(1)} %get-tuple-element.167, s32[]{:T(128)S(6)} %select_n.18), kind=kLoop, calls=%fused_computation.8.clone.1 | loop fusion | flops 11 | bytes 28 | tf_op jit(solution)/shard_map/while/body/eval_jaxpr/reduce_sum | solution.py:22
  86.3 0.8 fusion.25
  87.1 0.7 compare_convert_fusion.2
  87.7 0.1 multiply_subtract_fusion.2
  87.8 0.6 dynamic_slice.35
  90.3 1.3 %fusion.24 = f32[]{:T(128)} fusion(s32[]{:T(128)} %bitcast.36, f32[4,4]{0,1:T(4,128)S(1)} %get-tuple-element.167, s32[]{:T(128)S(6)} %select_n.18), kind=kLoop, calls=%fused_computation.8.clone.1 | loop fusion | flops 11 | bytes 28 | tf_op jit(solution)/shard_map/while/body/eval_jaxpr/reduce_sum | solution.py:22
  92.2 0.8 fusion.25
  93.0 0.7 compare_convert_fusion.2
  93.7 0.1 multiply_subtract_fusion.2
  93.8 0.6 dynamic_slice.35
  96.3 1.3 %fusion.24 = f32[]{:T(128)} fusion(s32[]{:T(128)} %bitcast.36, f32[4,4]{0,1:T(4,128)S(1)} %get-tuple-element.167, s32[]{:T(128)S(6)} %select_n.18), kind=kLoop, calls=%fused_computation.8.clone.1 | loop fusion | flops 11 | bytes 28 | tf_op jit(solution)/shard_map/while/body/eval_jaxpr/reduce_sum | solution.py:22
  98.2 0.8 fusion.25
  99.0 0.7 compare_convert_fusion.2
  99.7 0.1 multiply_subtract_fusion.2
  99.7 0.6 dynamic_slice.35
  102.3 1.3 %fusion.24 = f32[]{:T(128)} fusion(s32[]{:T(128)} %bitcast.36, f32[4,4]{0,1:T(4,128)S(1)} %get-tuple-element.167, s32[]{:T(128)S(6)} %select_n.18), kind=kLoop, calls=%fused_computation.8.clone.1 | loop fusion | flops 11 | bytes 28 | tf_op jit(solution)/shard_map/while/body/eval_jaxpr/reduce_sum | solution.py:22
  104.2 0.8 fusion.25
  105.0 0.7 compare_convert_fusion.2
  105.6 0.1 multiply_subtract_fusion.2
  105.7 0.0 copy-done.1
  105.7 0.0 copy-start.2
  105.7 2.5 %fusion.7 = bf16[1,128,1280]{2,0,1:T(2,128)(2,1)S(1)} fusion(bf16[4,128,1280]{2,1,0:T(8,128)(2,1)S(1)} %copy-done.1, f32[4]{0:T(128)S(1)} %reduce_sum.22), kind=kOutput, calls=%fused_computation.13 | convolution fusion | flops 7864320 | bytes 1638416 | tf_op jit(solution)/shard_map/k,ktc->tc/dot_general | solution.py:43
  108.3 2.9 %fusion.10 = f32[896,1280]{1,0:T(8,128)} fusion(bf16[1,128,1280]{2,0,1:T(2,128)(2,1)S(1)} %fusion.7, bf16[128,3584]{1,0:T(8,128)(2,1)S(1)} %copy-done, s32[]{:T(128)S(6)} %select_n.15), kind=kOutput, calls=%fused_computation.17 | convolution fusion | flops 293601280 | bytes 5472260 | tf_op jit(solution)/shard_map/dot_general | solution.py:46
  111.2 0.0 copy-done.2
  (2 shorter events, 0.0 us)
Async XLA Ops:
  7.2 23.3 %copy-start = (bf16[128,3584]{1,0:T(8,128)(2,1)S(1)}, bf16[128,3584]{1,0:T(8,128)(2,1)}, u32[]{:S(2)}) copy-start(bf16[128,3584]{1,0:T(8,128)(2,1)} %param.5) | copy-start | bytes 2752516
  7.2 23.3 %all-gather.2.cloned.1.call-start = ((), (), s32[]{:S(2)}) async-start(), calls=%async_computation | async-start | bytes 1638400 | tf_op jit(solution)/shard_map/all_gather | solution.py:37
  34.4 47.5 %copy-start.3 = (s32[4]{0:T(128)S(1)}, s32[4]{0:T(128)}, u32[]{:S(2)}) copy-start(s32[4]{0:T(128)} %param.7) | copy-start | bytes 52
  34.4 71.4 %copy-start.1 = (bf16[4,128,1280]{2,1,0:T(8,128)(2,1)S(1)}, bf16[4,128,1280]{2,1,0:T(8,128)(2,1)}, u32[]{:S(2)}) copy-start(bf16[4,128,1280]{2,1,0:T(8,128)(2,1)} %all-gather.2.cloned.1.call-done) | copy-start | bytes 3932164
  105.7 5.5 %copy-start.2 = (f32[4]{0:T(128)}, f32[4]{0:T(128)S(1)}, u32[]{:S(2)}) copy-start(f32[4]{0:T(128)S(1)} %reduce_sum.22) | copy-start | bytes 52
Sparse Core Ops, SparseCore 0:
  9.5 20.8 all-gather.1

commit v2 on v0

--- a/solution.py
+++ b/solution.py
@@ -38,7 +38,7 @@
     row_grads = task_grads(acts_rows, everyone)
     flat = row_grads.reshape(total_tasks, -1)
     partial_gram = jnp.dot(flat, flat.T, preferred_element_type=jnp.float32)
-    gram = lax.psum(partial_gram, ("task", "param"))
+    gram = jnp.sum(lax.all_gather(partial_gram, ("task", "param")), axis=0)
     weights = pcgrad_weights(gram, order)
     combined = jnp.einsum(
         "k,ktc->tc", weights, everyone.astype(jnp.float32), precision=lax.Precision.HIGHEST

time: 131 us -> 159 us (1.21)
  blocking collectives: 39.3 us -> 67.7 us
    all_gather x0 -> x1, blocking collectives: none -> 67.7 us  [shards(): gram = jnp.sum(lax.all_gather(partial_gram, ('task', 'param')), axis=0)]
    psum x1 -> x0, blocking collectives: 39.3 us -> none  [shards(): gram = lax.psum(partial_gram, ('task', 'param'))]
where the time goes in v2:
time: 159 us; the launch traced here: 158 us
  blocking collectives  67.7 us (43%)
  matrix products  32.5 us (20%)
  waiting for transfers between devices  23.2 us (15%)
  between operations  14.1 us (9%)
  loops' own time  10.4 us (7%)
  other arithmetic  8.14 us (5%)
  local copies, waits for them, and re-layouts  2.45 us (2%)
    all_gather x1, blocking collectives, shards(): gram = jnp.sum(lax.all_gather(partial_gram, ('task', 'param')), axis=0)  67.7 us
    all_gather x1, waiting for transfers between devices, shards(): everyone = lax.all_gather(out_grads, 'task', axis=0, tiled=True)  22.5 us
    dot_general x1, matrix products, shards(): partial_gram = jnp.dot(flat, flat.T, preferred_element_type=jnp.float32)  20.1 us
    another operation x1, loops' own time, pcgrad_weights(): mix = lax.fori_loop(0, count, turn, jnp.eye(count, dtype=jnp.float32))  10.4 us
    reduce_sum x4, other arithmetic, turn(): scale = jnp.sum(column * onehot) + 1e-06  5.13 us
    dot_general x1, matrix products, task_grads(): jnp.einsum('td,ktc->kdc', acts_part, blocks, preferred_element_type=jnp.f...  3.88 us
  transfers between devices with their start and end apart: 1, of which 1 were waited for; matrix products, arithmetic and copies ran while one was open for 0% of the time, Pallas kernels for 0%

profile of v2, /device:TPU:0, one launch (start us, length us, event | category | flops | bytes accessed | tf_op | source)
XLA Modules:
  0.0 158.5 jit_solution(10263161753390968753)
XLA Ops:
  7.2 0.0 copy-start
  7.2 0.0 all-gather.4.cloned.1.call-start
  7.2 0.7 all-gather.4.cloned.1.call-update
  7.9 22.5 %all-gather.4.cloned.1.call-done = bf16[4,128,1280]{2,1,0:T(8,128)(2,1)} async-done(((bf16[1,128,1280]{2,1,0:T(8,128)(2,1)}), bf16[4,128,1280]{2,1,0:T(8,128)(2,1)}) %all-gather.4.cloned.1.call-update) | async-done | bytes 1310736 | tf_op jit(solution)/shard_map/all_gather | solution.py:37
  30.5 0.0 copy-done
  30.5 3.9 %convolution_convert_fusion = bf16[896,4,1280]{2,0,1:T(8,128)(2,1)S(1)} fusion(bf16[4,128,1280]{2,1,0:T(8,128)(2,1)} %all-gather.4.cloned.1.call-done, bf16[128,3584]{1,0:T(8,128)(2,1)S(1)} %copy-done, s32[]{:T(128)S(6)} %select_n.15), kind=kOutput, calls=%fused_computation.10 | convolution fusion | flops 1178992640 | bytes 10715140 | tf_op jit(solution)/shard_map/td,ktc->kdc/dot_general | solution.py:8
  34.4 0.0 copy-start.3
  34.4 0.0 copy-start.1
  34.4 20.1 %fusion.9 = f32[1,4,4]{2,1,0:T(4,128)S(1)} fusion(bf16[896,4,1280]{2,0,1:T(8,128)(2,1)S(1)} %convolution_convert_fusion), kind=kOutput, calls=%fused_computation.15 | convolution fusion | flops 36700160 | bytes 9175104 | tf_op jit(solution)/shard_map/dot_general | solution.py:40
  54.4 67.7 %all-gather.1 = f32[32,4,4]{2,1,0:T(4,128)S(1)} all-gather(f32[1,4,4]{2,1,0:T(4,128)S(1)} %fusion.9), channel_id=2, replica_groups=mesh['task'=4,'param'=8] {'task','param'}, dimensions={0}, use_global_device_ids=true | all-gather | bytes 2112 | tf_op jit(solution)/shard_map/all_gather | solution.py:41
  122.2 0.1 copy.5
  122.3 0.0 copy-done.3
  122.3 23.9 %while.14 = (s32[]{:T(128)}, f32[4,4]{1,0:T(4,128)S(1)}, s32[4]{0:T(128)S(1)}, f32[4,4]{0,1:T(4,128)S(1)}, s32[]{:T(128)}, /*index=5*/s32[]{:T(128)}, s32[]{:T(128)}, f32[]{:T(128)}) while((s32[]{:T(128)}, f32[4,4]{1,0:T(4,128)S(1)}, s32[4]{0:T(128)S(1)}, f32[4,4]{0,1:T(4,128)S(1)}, s32[]{:T(128)}, /*index=5*/s32[]{:T(128)}, ...), condition=%wide.region_3.0_spmd.clone, body=%wide.region_1.0_spmd.clone.sunk | while | flops 273 | bytes 2939 | solution.py:26
  122.3 0.6 dynamic_slice.35
  124.8 1.3 fusion.24
  126.7 0.8 fusion.25
  127.5 0.7 compare_convert_fusion.2
  128.2 0.1 multiply_subtract_fusion.2
  128.2 0.6 dynamic_slice.35
  130.8 1.3 fusion.24
  132.7 0.8 fusion.25
  133.5 0.7 compare_convert_fusion.2
  134.1 0.1 multiply_subtract_fusion.2
  134.2 0.6 dynamic_slice.35
  136.7 1.3 fusion.24
  138.6 0.8 fusion.25
  139.4 0.7 compare_convert_fusion.2
  140.1 0.1 multiply_subtract_fusion.2
  140.2 0.6 dynamic_slice.35
  142.7 1.3 fusion.24
  144.6 0.8 fusion.25
  145.4 0.7 compare_convert_fusion.2
  146.1 0.1 multiply_subtract_fusion.2
  146.2 0.0 copy-done.1
  146.2 0.0 copy-start.2
  146.2 2.5 %fusion.7 = bf16[1,128,1280]{2,0,1:T(2,128)(2,1)S(1)} fusion(bf16[4,128,1280]{2,1,0:T(8,128)(2,1)S(1)} %copy-done.1, f32[4]{0:T(128)S(1)} %reduce_sum.32), kind=kOutput, calls=%fused_computation.13 | convolution fusion | flops 7864320 | bytes 1638416 | tf_op jit(solution)/shard_map/k,ktc->tc/dot_general | solution.py:43
  148.7 2.9 %fusion.10 = f32[896,1280]{1,0:T(8,128)} fusion(bf16[1,128,1280]{2,0,1:T(2,128)(2,1)S(1)} %fusion.7, bf16[128,3584]{1,0:T(8,128)(2,1)S(1)} %copy-done, s32[]{:T(128)S(6)} %select_n.15), kind=kOutput, calls=%fused_computation.17 | convolution fusion | flops 293601280 | bytes 5472260 | tf_op jit(solution)/shard_map/dot_general | solution.py:46
  151.6 0.0 copy-done.2
  (3 shorter events, 0.1 us)
Async XLA Ops:
  7.2 23.3 %copy-start = (bf16[128,3584]{1,0:T(8,128)(2,1)S(1)}, bf16[128,3584]{1,0:T(8,128)(2,1)}, u32[]{:S(2)}) copy-start(bf16[128,3584]{1,0:T(8,128)(2,1)} %param.5) | copy-start | bytes 2752516
  7.2 23.3 %all-gather.4.cloned.1.call-start = ((), (), s32[]{:S(2)}) async-start(), calls=%async_computation | async-start | bytes 1638400 | tf_op jit(solution)/shard_map/all_gather | solution.py:37
  34.4 87.9 %copy-start.3 = (s32[4]{0:T(128)S(1)}, s32[4]{0:T(128)}, u32[]{:S(2)}) copy-start(s32[4]{0:T(128)} %param.7) | copy-start | bytes 52
  34.4 111.8 %copy-start.1 = (bf16[4,128,1280]{2,1,0:T(8,128)(2,1)S(1)}, bf16[4,128,1280]{2,1,0:T(8,128)(2,1)}, u32[]{:S(2)}) copy-start(bf16[4,128,1280]{2,1,0:T(8,128)(2,1)} %all-gather.4.cloned.1.call-done) | copy-start | bytes 3932164
  146.2 5.5 %copy-start.2 = (f32[4]{0:T(128)}, f32[4]{0:T(128)S(1)}, u32[]{:S(2)}) copy-start(f32[4]{0:T(128)S(1)} %reduce_sum.32) | copy-start | bytes 52
Sparse Core Ops, SparseCore 0:
  9.5 20.8 all-gather.3
